TPU v7x, 32 devices: a whole 2x2x4 slice. The times are simulated.
32 devices in a mesh: px: 4 (over y, x), py: 8 (over z, core).
Axes of the slice: x: 2, y: 2, z: 4, core: 2. Of those that a mesh axis runs over, the one named last changes fastest.
Arguments:
- photons: float32 [1024, 128], P(('px', 'py')), may hold values from 50 to 1000
- halo_cells: int32 [1024, 128], P(('px', 'py')), may hold values from 0 to 1769471
- halo_counts: int32 [1024], P(('px', 'py')), may hold values from 1 to 128
- owners: int32 [1024, 1], P(('px', 'py')), may hold values from 0 to 7; in each aligned block of 32 rows (0 to 31, 32 to 63, ...) at most 4 rows name the same one
- density: float32 [384, 384, 384], P('px', 'py'), may hold values from 0.02 to 50
Outputs:
- fraction: float32 [384, 384, 384], P('px', 'py')
Inputs may be any that keep to these rules, and one draw needn't show every extreme that they name: The halos of a block all lie in pencil owners[b] of the block's own slab. Among the 32 blocks of one device no owner appears more than 4 times, a bound that some block reaches. Slots at or past halo_counts[b] are not live and carry arbitrary values. `halo_cells`: A cell index within the owner pencil is (x * 48 + y) * 384 + z with x, y, z local to that pencil.
All inputs are finite; a program needn't handle non-finite values.
Results may differ from a plain program's by a relative error of at most 0.0003.
Values sent between devices are 32-bit elements; how exact they have to be, the bound alone decides.
A program may use at most 192 MiB of HBM per device.

v0:
```python
import jax
import jax.numpy as jnp
from jax import lax
from jax.sharding import PartitionSpec as P

NG = 384
SLOTS = 128
RADIUS = 20


def product(form, left, right):
    return jnp.einsum(form, left, right, precision=lax.Precision.HIGHEST)


def rotate(form, real_part, imag_part, cos_table, sin_table, direction):
    signed_sin = direction * sin_table
    first = product(form, real_part + imag_part, cos_table)
    second = product(form, real_part, signed_sin - cos_table)
    third = product(form, imag_part, cos_table + signed_sin)
    return (first - third, first + second)


def tables(length):
    index_row = jnp.arange(length, dtype=jnp.int32)
    angle = (index_row[:, None] * index_row[None, :] % length).astype(jnp.float32) * (
        2.0 * jnp.pi / length
    )
    return (jnp.cos(angle), jnp.sin(angle))


def signed_frequency(index_values):
    return jnp.where(index_values < NG // 2, index_values, index_values - NG).astype(jnp.float32)


def top_hat(freq_x, freq_y, freq_z):
    radial = jnp.sqrt(freq_x * freq_x + freq_y * freq_y + freq_z * freq_z) * (
        2.0 * jnp.pi * RADIUS / NG
    )
    safe = jnp.where(radial > 0, radial, 1.0)
    value = 3.0 * (jnp.sin(safe) - safe * jnp.cos(safe)) / (safe * safe * safe)
    return jnp.where(radial > 0, value, 1.0)


def paint(photon_rows, cell_rows, live_rows, cell_total):
    weights = jnp.where(live_rows, photon_rows, 0.0)
    empty = jnp.zeros((cell_total,), jnp.float32)
    return empty.at[cell_rows.reshape(-1)].add(weights.reshape(-1))


def on_device(photons, halo_cells, halo_counts, owners, density):
    rows_x, rows_y = (density.shape[0], density.shape[1])
    cell_total = rows_x * rows_y * NG
    count_x = lax.axis_size("px")
    count_y = lax.axis_size("py")
    place_y = lax.axis_index("py")
    slot_index = jnp.arange(SLOTS, dtype=jnp.int32)[None, :]
    all_photons, all_cells, all_counts, all_owners = (
        lax.all_gather(photons, "py", axis=0, tiled=True),
        lax.all_gather(halo_cells, "py", axis=0, tiled=True),
        lax.all_gather(halo_counts, "py", axis=0, tiled=True),
        lax.all_gather(owners, "py", axis=0, tiled=True),
    )
    live_rows = (slot_index < all_counts[:, None]) & (all_owners == place_y)
    painted = paint(all_photons, all_cells, live_rows, cell_total)
    cos_full, sin_full = tables(NG)
    field_rows = painted.reshape(rows_x * rows_y, NG)
    density_rows = density.reshape(rows_x * rows_y, NG)
    spec_real, spec_imag = rotate("az,zk->ka", field_rows, density_rows, cos_full, sin_full, -1.0)
    cos_y = cos_full.reshape(count_y, rows_y, NG)
    sin_y = sin_full.reshape(count_y, rows_y, NG)
    cos_x = cos_full.reshape(count_x, rows_x, NG)
    sin_x = sin_full.reshape(count_x, rows_x, NG)
    freq_all = signed_frequency(jnp.arange(NG, dtype=jnp.int32))
    devices_all = count_x * count_y
    slab_planes = NG // devices_all
    sent = (
        spec_real.reshape(devices_all, slab_planes, rows_x * rows_y),
        spec_imag.reshape(devices_all, slab_planes, rows_x * rows_y),
    )
    got_real, got_imag = (
        lax.all_to_all(sent[0], ("px", "py"), split_axis=0, concat_axis=2, tiled=True),
        lax.all_to_all(sent[1], ("px", "py"), split_axis=0, concat_axis=2, tiled=True),
    )
    got_real = got_real.reshape(slab_planes, count_x, count_y, rows_x, rows_y)
    got_imag = got_imag.reshape(slab_planes, count_x, count_y, rows_x, rows_y)
    plane_real, plane_imag = rotate("kiqxl,qlm->kixm", got_real, got_imag, cos_y, sin_y, -1.0)
    full_real, full_imag = rotate("kixm,ixn->kmn", plane_real, plane_imag, cos_x, sin_x, -1.0)
    freq_z = signed_frequency(
        lax.axis_index(("px", "py")) * slab_planes + jnp.arange(slab_planes, dtype=jnp.int32)
    )
    window = top_hat(freq_z[:, None, None], freq_all[None, :, None], freq_all[None, None, :])
    full_real = full_real * window
    full_imag = full_imag * window
    plane_real, plane_imag = rotate("kmn,ixn->kmix", full_real, full_imag, cos_x, sin_x, 1.0)
    back_real, back_imag = rotate("kmix,qlm->iqkxl", plane_real, plane_imag, cos_y, sin_y, 1.0)
    sent = (
        back_real.reshape(devices_all, slab_planes, rows_x * rows_y),
        back_imag.reshape(devices_all, slab_planes, rows_x * rows_y),
    )
    got_real, got_imag = (
        lax.all_to_all(sent[0], ("px", "py"), split_axis=0, concat_axis=1, tiled=True),
        lax.all_to_all(sent[1], ("px", "py"), split_axis=0, concat_axis=1, tiled=True),
    )
    got_real = got_real.reshape(NG, rows_x * rows_y)
    got_imag = got_imag.reshape(NG, rows_x * rows_y)
    final_real, final_imag = rotate("ka,kz->az", got_real, got_imag, cos_full, sin_full, 1.0)
    scale = 1.0 / (float(NG) * float(NG) * float(NG))
    photon_smooth = final_real * scale
    density_smooth = final_imag * scale
    fraction = jnp.clip(photon_smooth / jnp.maximum(density_smooth, 0.5), 0.0, 1.0)
    return fraction.reshape(rows_x, rows_y, NG)


def solution(mesh):
    placed = (
        P(("px", "py"), None),
        P(("px", "py"), None),
        P(("px", "py")),
        P(("px", "py"), None),
        P("px", "py", None),
    )
    return jax.shard_map(
        on_device, mesh=mesh, in_specs=placed, out_specs=P("px", "py", None), check_vma=False
    )
```

profile of v0, /device:TPU:0, one launch (start us, length us, event | category | flops | bytes accessed | tf_op | source)
XLA Modules:
  0.0 1580.6 jit_solution(1984231770731450605)
XLA Ops:
  42.8 174.8 %scatter_custom_fusion = f32[1769472]{0:T(1024)} fusion(s32[32768]{0:T(1024)S(1)} %bitcast.192, f32[32768]{0:T(1024)S(1)} %select_bitcast_fusion, f32[]{:T(128)} %constant.19.clone.1), kind=kCustom, calls=%fused_computation.47 | custom fusion | flops 32768 | bytes 7077892 | tf_op jit(solution)/shard_map/scatter-add | solution.py:47
  226.4 24.8 %fusion.29 = f32[384,4608]{1,0:T(8,128)S(1)} fusion(f32[4608,384]{1,0:T(8,128)} %reshape.184, f32[4608,384]{1,0:T(8,128)} %bitcast.189), kind=kOutput, calls=%fused_computation.45 | convolution fusion | flops 8156823552 | bytes 21233664 | tf_op jit(solution)/shard_map/az,zk->ka/dot_general | solution.py:12
  254.1 26.1 %convolution_add_fusion.1 = f32[384,4608]{1,0:T(8,128)} fusion(f32[384,4608]{1,0:T(8,128)S(1)} %fusion.29, f32[4608,384]{1,0:T(8,128)S(1)} %copy-done.6), kind=kOutput, calls=%fused_computation.11 | convolution fusion | flops 8157118464 | bytes 21233664 | tf_op jit(solution)/shard_map/az,zk->ka/dot_general | solution.py:12
  292.1 29.4 %convolution_subtract_fusion.1 = f32[384,4608]{1,0:T(8,128)} fusion(f32[384,4608]{1,0:T(8,128)} %copy-done.3, f32[4608,384]{1,0:T(8,128)} %bitcast.190), kind=kOutput, calls=%fused_computation.12 | convolution fusion | flops 8157118464 | bytes 21233664 | tf_op jit(solution)/shard_map/az,zk->ka/dot_general | solution.py:12
  329.5 169.9 %all-to-all-done.1 = f32[32,12,4608]{2,1,0:T(8,128)} async-done(((f32[32,12,4608]{2,1,0:T(8,128)}), f32[32,12,4608]{2,1,0:T(8,128)}, u32[]{:S(2)}, u32[]{:S(2)}) %all-to-all-start.1) | async-done | bytes 7077920 | tf_op jit(solution)/shard_map/all_to_all | solution.py:82
  519.2 26.0 %reshape.189 = f32[12,4,8,96,48]{4,3,2,1,0:T(8,128)} reshape(f32[1,12,32,4608]{3,2,1,0:T(8,128)} %copy.16) | data formatting | bytes 14155776 | tf_op jit(solution)/shard_map/reshape | solution.py:85
  545.3 165.4 %all-to-all-done = f32[32,12,4608]{2,1,0:T(8,128)} async-done(((f32[32,12,4608]{2,1,0:T(8,128)}), f32[32,12,4608]{2,1,0:T(8,128)}, u32[]{:S(2)}, u32[]{:S(2)}) %all-to-all-start) | async-done | bytes 7077920 | tf_op jit(solution)/shard_map/all_to_all | solution.py:81
  736.5 26.2 %fusion.53 = f32[12,4,96,384,1]{3,2,4,1,0:T(8,128)} fusion(f32[12,4,8,96,48]{4,3,2,1,0:T(8,128)} %reshape.189, s32[8,48]{1,0:T(8,128)S(1)} %multiply_add_fusion), kind=kOutput, calls=%fused_computation.69 | convolution fusion | flops 8155348992 | bytes 14157312 | tf_op jit(solution)/shard_map/kiqxl,qlm->kixm/dot_general | solution.py:12
  762.7 27.8 %fusion = f32[12,4,96,384,1]{3,2,4,1,0:T(8,128)} fusion(f32[12,4,8,96,48]{4,3,2,1,0:T(8,128)S(1)} %copy-done, f32[12,4,8,96,48]{4,3,2,1,0:T(8,128)} %reshape.189, s32[8,48]{1,0:T(8,128)S(1)} %multiply_add_fusion), kind=kOutput, calls=%fused_computation.1 | convolution fusion | flops 8156823552 | bytes 21235200 | tf_op jit(solution)/shard_map/kiqxl,qlm->kixm/dot_general | solution.py:12
  790.5 22.9 %fusion.51 = f32[12,4,96,384,1]{3,2,4,1,0:T(8,128)} fusion(f32[12,4,8,96,48]{4,3,2,1,0:T(8,128)S(1)} %copy-done, s32[8,48]{1,0:T(8,128)S(1)} %multiply_add_fusion), kind=kOutput, calls=%fused_computation.67 | convolution fusion | flops 8155348992 | bytes 14157312 | tf_op jit(solution)/shard_map/kiqxl,qlm->kixm/dot_general | solution.py:12
  813.4 25.1 %fusion.27 = f32[12,384,384,1]{2,1,3,0:T(8,128)S(1)} fusion(f32[12,4,96,384,1]{3,2,4,1,0:T(8,128)} %fusion.53, f32[12,4,96,384,1]{3,2,4,1,0:T(8,128)} %fusion, f32[12,4,96,384,1]{3,2,4,1,0:T(8,128)} %fusion.51, s32[4,96]{1,0:T(4,128)S(1)} %multiply_add_fusion.1), kind=kOutput, calls=%fused_computation.43 | convolution fusion | flops 8160362496 | bytes 28313088 | tf_op jit(solution)/shard_map/kixm,ixn->kmn/dot_general | solution.py:12
  838.5 50.9 %fusion.21 = f32[12,384,384]{2,1,0:T(8,128)S(1)} fusion(f32[12,384,384,1]{2,1,3,0:T(8,128)S(1)} %fusion.27, f32[384]{0:T(512)S(1)} %fusion.197, f32[12,384]{1,0:T(8,128)S(1)} %broadcast_add_fusion, f32[12,4,96,384,1]{3,2,4,1,0:T(8,128)} %fusion.53, f32[12,4,96,384,1]{3,2,4,1,0:T(8,128)S(1)} %copy-done.7, f32[4,96,384,1]{2,1,0,3:T(8,128)S(1)} %fusion.272), kind=kOutput, calls=%fused_computation.33 | convolution fusion | flops 8178499584 | bytes 28921344 | tf_op jit(solution)/shard_map/kixm,ixn->kmn/dot_general | solution.py:12
  889.5 20.6 %fusion.11 = f32[12,384,4,96]{1,3,2,0:T(8,128)} fusion(f32[12,384,384]{2,1,0:T(8,128)S(1)} %fusion.21, s32[4,96]{1,0:T(4,128)S(1)} %multiply_add_fusion.1), kind=kOutput, calls=%fused_computation.22 | convolution fusion | flops 8155201536 | bytes 14157312 | tf_op jit(solution)/shard_map/kmn,ixn->kmix/dot_general | solution.py:12
  910.1 50.8 %fusion.22 = f32[12,384,384]{2,1,0:T(8,128)S(1)} fusion(f32[12,384,384,1]{2,1,3,0:T(8,128)} %copy-done.9, f32[384]{0:T(512)S(1)} %fusion.197, f32[12,384]{1,0:T(8,128)S(1)} %broadcast_add_fusion, f32[12,4,96,384,1]{3,2,4,1,0:T(8,128)S(1)} %bitcast.186, f32[12,4,96,384,1]{3,2,4,1,0:T(8,128)S(1)} %copy-done.7, f32[4,96,384,1]{2,1,0,3:T(8,128)S(1)} %fusion.274), kind=kOutput, calls=%fused_computation.35 | convolution fusion | flops 8178499584 | bytes 28921344 | tf_op jit(solution)/shard_map/kixm,ixn->kmn/dot_general | solution.py:12
  978.3 20.0 %fusion.9 = f32[12,384,4,96]{1,3,2,0:T(8,128)S(1)} fusion(f32[12,384,384]{2,1,0:T(8,128)} %copy-done.8, s32[4,96]{1,0:T(4,128)S(1)} %multiply_add_fusion.1), kind=kOutput, calls=%fused_computation.20 | convolution fusion | flops 8155201536 | bytes 14157312 | tf_op jit(solution)/shard_map/kmn,ixn->kmix/dot_general | solution.py:12
  998.3 24.4 %fusion.19 = f32[8,48,12,4,96]{4,1,3,2,0:T(8,128)S(1)} fusion(f32[12,384,4,96]{1,3,2,0:T(8,128)S(1)} %fusion.13, f32[12,384,4,96]{1,3,2,0:T(8,128)S(1)} %fusion.9, f32[12,384,4,96]{1,3,2,0:T(8,128)} %fusion.11, s32[8,48]{1,0:T(8,128)S(1)} %multiply_add_fusion), kind=kOutput, calls=%fused_computation.30 | convolution fusion | flops 8160362496 | bytes 28313088 | tf_op jit(solution)/shard_map/kmix,qlm->iqkxl/dot_general | solution.py:12
  1026.4 24.8 %add_bitcast_fusion = f32[4,8,12,96,48]{3,4,0,2,1:T(8,128)} fusion(f32[8,48,12,4,96]{4,1,3,2,0:T(8,128)S(1)} %fusion.19, f32[12,384,4,96]{1,3,2,0:T(8,128)S(1)} %fusion.13, f32[12,384,4,96]{1,3,2,0:T(8,128)} %fusion.11, s32[8,48]{1,0:T(8,128)S(1)} %multiply_add_fusion), kind=kOutput, calls=%fused_computation.5 | convolution fusion | flops 8158740480 | bytes 28313088 | tf_op jit(solution)/shard_map/kmix,qlm->iqkxl/dot_general | solution.py:12
  1065.9 19.0 %reshape.239 = f32[32,12,4608]{2,1,0:T(8,128)} reshape(f32[4,8,12,96,48]{4,3,2,1,0:T(8,128)} %copy.43) | data formatting | bytes 14155776 | tf_op jit(solution)/shard_map/reshape | solution.py:98
  1089.1 31.1 %subtract_bitcast_fusion = f32[4,8,12,96,48]{3,4,0,2,1:T(8,128)} fusion(f32[8,48,12,4,96]{4,1,3,2,0:T(8,128)} %copy-done.4, f32[12,384,4,96]{1,3,2,0:T(8,128)} %copy-done.2, f32[12,384,4,96]{1,3,2,0:T(8,128)} %copy-done.5, s32[8,48]{1,0:T(8,128)S(1)} %multiply_add_fusion), kind=kOutput, calls=%fused_computation.6 | convolution fusion | flops 8158740480 | bytes 28313088 | tf_op jit(solution)/shard_map/kmix,qlm->iqkxl/dot_general | solution.py:12
  1134.9 19.0 %reshape.238 = f32[32,12,4608]{2,1,0:T(8,128)} reshape(f32[4,8,12,96,48]{4,3,2,1,0:T(8,128)} %copy.42) | data formatting | bytes 14155776 | tf_op jit(solution)/shard_map/reshape | solution.py:97
  1154.0 142.4 %all-to-all-done.3 = f32[32,12,4608]{2,1,0:T(8,128)} async-done(((f32[32,12,4608]{2,1,0:T(8,128)}), f32[32,12,4608]{2,1,0:T(8,128)}, u32[]{:S(2)}, u32[]{:S(2)}) %all-to-all-start.3) | async-done | bytes 7077920 | tf_op jit(solution)/shard_map/all_to_all | solution.py:102
  1308.3 199.0 %all-to-all-done.2 = f32[32,12,4608]{2,1,0:T(8,128)} async-done(((f32[32,12,4608]{2,1,0:T(8,128)}), f32[32,12,4608]{2,1,0:T(8,128)}, u32[]{:S(2)}, u32[]{:S(2)}) %all-to-all-start.2) | async-done | bytes 7077920 | tf_op jit(solution)/shard_map/all_to_all | solution.py:101
  1515.5 23.8 %fusion.23 = f32[4608,384]{1,0:T(8,128)S(1)} fusion(f32[384,4608]{1,0:T(8,128)} %reshape.191, f32[384,4608]{1,0:T(8,128)} %reshape.193), kind=kOutput, calls=%fused_computation.39 | convolution fusion | flops 8156823552 | bytes 21233664 | tf_op jit(solution)/shard_map/ka,kz->az/dot_general | solution.py:12
  1558.1 22.3 %divide_clamp_fusion = f32[4608,384]{1,0:T(8,128)} fusion(f32[4608,384]{1,0:T(8,128)S(1)} %fusion.4, f32[4608,384]{1,0:T(8,128)S(1)} %fusion.23, f32[384,4608]{1,0:T(8,128)S(1)} %bitcast.188), kind=kOutput, calls=%fused_computation.38 | convolution fusion | flops 8162279424 | bytes 28311552 | tf_op jit(solution)/shard_map/ka,kz->az/dot_general | solution.py:12
  (64 shorter events, 212.8 us)
Async XLA Ops:
  226.4 27.8 %copy-start.6 = (f32[4608,384]{1,0:T(8,128)S(1)}, f32[4608,384]{1,0:T(8,128)}, u32[]{:S(2)}) copy-start(f32[4608,384]{1,0:T(8,128)} %reshape.184) | copy-start | bytes 21233668
  251.2 2.9 copy-start.3
  288.2 211.2 %all-to-all-start.1 = ((f32[32,12,4608]{2,1,0:T(8,128)}), f32[32,12,4608]{2,1,0:T(8,128)}, u32[]{:S(2)}, u32[]{:S(2)}) async-start(f32[32,12,4608]{2,1,0:T(8,128)} %reshape.188), calls=%async_computation.1 | async-start | bytes 18874368 | tf_op jit(solution)/shard_map/all_to_all | solution.py:82
  499.4 211.3 %all-to-all-start = ((f32[32,12,4608]{2,1,0:T(8,128)}), f32[32,12,4608]{2,1,0:T(8,128)}, u32[]{:S(2)}, u32[]{:S(2)}) async-start(f32[32,12,4608]{2,1,0:T(8,128)} %reshape.186), calls=%async_computation | async-start | bytes 18874368 | tf_op jit(solution)/shard_map/all_to_all | solution.py:81
  736.5 26.2 %copy-start = (f32[12,4,8,96,48]{4,3,2,1,0:T(8,128)S(1)}, f32[12,4,8,96,48]{4,3,2,1,0:T(8,128)}, u32[]{:S(2)}) copy-start(f32[12,4,8,96,48]{4,3,2,1,0:T(8,128)} %reshape.187) | copy-start | bytes 21233668
  813.4 25.1 %copy-start.7 = (f32[12,4,96,384,1]{3,2,4,1,0:T(8,128)S(1)}, f32[12,4,96,384,1]{3,2,4,1,0:T(8,128)}, u32[]{:S(2)}) copy-start(f32[12,4,96,384,1]{3,2,4,1,0:T(8,128)} %fusion) | copy-start | bytes 21233668
  813.4 96.7 %slice-start = ((s8[7077888]{0:T(1024)(128)(4,1)}), s8[4194304]{0:T(1024)(128)(4,1)S(1)}, s32[]{:S(2)}) async-start(s8[7077888]{0:T(1024)(128)(4,1)} %bitcast.185), calls=%async_computation.4 | async-start | bytes 8388608
  838.5 50.9 %copy-start.9 = (f32[12,384,384,1]{2,1,3,0:T(8,128)}, f32[12,384,384,1]{2,1,3,0:T(8,128)S(1)}, u32[]{:S(2)}) copy-start(f32[12,384,384,1]{2,1,3,0:T(8,128)S(1)} %fusion.27) | copy-start | bytes 21233668
  838.5 71.6 %slice-start.1 = ((s8[7077888]{0:T(1024)(128)(4,1)}), s8[2883584]{0:T(1024)(128)(4,1)S(1)}, s32[]{:S(2)}) async-start(s8[7077888]{0:T(1024)(128)(4,1)} %bitcast.185), calls=%async_computation.5 | async-start | bytes 5767168
  960.8 3.0 copy-start.8
  978.2 44.5 %copy-start.2 = (f32[12,384,4,96]{1,3,2,0:T(8,128)}, f32[12,384,4,96]{1,3,2,0:T(8,128)S(1)}, u32[]{:S(2)}) copy-start(f32[12,384,4,96]{1,3,2,0:T(8,128)S(1)} %fusion.13) | copy-start | bytes 21233668
  998.3 24.5 %copy-start.5 = (f32[12,384,4,96]{1,3,2,0:T(8,128)}, f32[12,384,4,96]{1,3,2,0:T(8,128)S(1)}, u32[]{:S(2)}) copy-start(f32[12,384,4,96]{1,3,2,0:T(8,128)S(1)} %fusion.9) | copy-start | bytes 21233668
  1022.7 3.7 copy-start.4
  1084.9 211.4 %all-to-all-start.3 = ((f32[32,12,4608]{2,1,0:T(8,128)}), f32[32,12,4608]{2,1,0:T(8,128)}, u32[]{:S(2)}, u32[]{:S(2)}) async-start(f32[32,12,4608]{2,1,0:T(8,128)} %reshape.239), calls=%async_computation.3 | async-start | bytes 18874368 | tf_op jit(solution)/shard_map/all_to_all | solution.py:102
  1296.3 211.0 %all-to-all-start.2 = ((f32[32,12,4608]{2,1,0:T(8,128)}), f32[32,12,4608]{2,1,0:T(8,128)}, u32[]{:S(2)}, u32[]{:S(2)}) async-start(f32[32,12,4608]{2,1,0:T(8,128)} %reshape.238), calls=%async_computation.2 | async-start | bytes 18874368 | tf_op jit(solution)/shard_map/all_to_all | solution.py:101
  1515.5 23.9 %copy-start.1 = (f32[384,4608]{1,0:T(8,128)S(1)}, f32[384,4608]{1,0:T(8,128)}, u32[]{:S(2)}) copy-start(f32[384,4608]{1,0:T(8,128)} %reshape.191) | copy-start | bytes 21233668
  1515.5 42.5 %slice-start.2 = ((s8[7077888]{0:T(1024)(128)(4,1)}), s8[4194304]{0:T(1024)(128)(4,1)S(1)}, s32[]{:S(2)}) async-start(s8[7077888]{0:T(1024)(128)(4,1)} %bitcast.187), calls=%async_computation.6 | async-start | bytes 8388608
  1539.4 18.7 %slice-start.3 = ((s8[7077888]{0:T(1024)(128)(4,1)}), s8[2883584]{0:T(1024)(128)(4,1)S(1)}, s32[]{:S(2)}) async-start(s8[7077888]{0:T(1024)(128)(4,1)} %bitcast.187), calls=%async_computation.7 | async-start | bytes 5767168
where the time goes:
time: 1590 us; the launch traced here: 1580 us
  waiting for transfers between devices  677 us (43%)
  matrix products  484 us (30%)
  local copies, waits for them, and re-layouts  184 us (12%)
  other arithmetic  180 us (11%)
  blocking collectives  39 us (2%)
    dot_general x18, matrix products, product(): return jnp.einsum(form, left, right, precision=lax.Precision.HIGHEST)  484 us
    all_to_all x1, waiting for transfers between devices, on_device(): lax.all_to_all(sent[0], ('px', 'py'), split_axis=0, concat_axis=1, tiled=...  199 us
    scatter-add x1, other arithmetic, paint(): return empty.at[cell_rows.reshape(-1)].add(weights.reshape(-1))  175 us
    all_to_all x1, waiting for transfers between devices, on_device(): lax.all_to_all(sent[1], ('px', 'py'), split_axis=0, concat_axis=2, tiled=...  170 us
    all_to_all x1, waiting for transfers between devices, on_device(): lax.all_to_all(sent[0], ('px', 'py'), split_axis=0, concat_axis=2, tiled=...  165 us
    all_to_all x1, waiting for transfers between devices, on_device(): lax.all_to_all(sent[1], ('px', 'py'), split_axis=0, concat_axis=1, tiled=...  142 us
    reshape x2, local copies, waits for them, and re-layouts, on_device(): back_imag.reshape(devices_all, slab_planes, rows_x * rows_y)  33.8 us
    reshape x2, local copies, waits for them, and re-layouts, on_device(): back_real.reshape(devices_all, slab_planes, rows_x * rows_y)  33.8 us
  transfers between devices with their start and end apart: 4, of which 4 were waited for; matrix products, arithmetic and copies ran while one was open for 10% of the time, Pallas kernels for 0%

commit v1 on v0

--- a/solution.py
+++ b/solution.py
@@ -79,7 +79,15 @@
     )
     got_real, got_imag = (
         lax.all_to_all(sent[0], ("px", "py"), split_axis=0, concat_axis=2, tiled=True),
-        lax.all_to_all(sent[1], ("px", "py"), split_axis=0, concat_axis=2, tiled=True),
+        jnp.concatenate(
+            lax.all_to_all(
+                jnp.stack(jnp.split(sent[1], lax.axis_size(("px", "py")), axis=0)),
+                ("px", "py"),
+                0,
+                0,
+            ),
+            axis=2,
+        ),
     )
     got_real = got_real.reshape(slab_planes, count_x, count_y, rows_x, rows_y)
     got_imag = got_imag.reshape(slab_planes, count_x, count_y, rows_x, rows_y)

time: 1590 us -> 1530 us (0.962)
  waiting for transfers between devices: 677 us -> 639 us
    all_to_all x1, waiting for transfers between devices: 170 us -> 119 us  [on_device(): lax.all_to_all(jnp.stack(jnp.split(sent[1], lax.axis_size(('px', 'py')),...]
    reshape x2 -> x1, local copies, waits for them, and re-layouts: 34 us -> 8.25 us  [on_device(): jnp.concatenate(lax.all_to_all(jnp.stack(jnp.split(sent[1], lax.axis_size...]
    another operation x0 -> x3, local copies, waits for them, and re-layouts: none -> 23.6 us  [the longest x1 15.2 us: on_device(): got_imag = got_imag.reshape(slab_planes, count_x, count_y, rows_x, rows_y)]
  transfers between devices with their start and end apart: 4 -> 4, of which waited for: 4 -> 4; matrix products, arithmetic and copies ran while one was open for 10% -> 9% of each run, Pallas kernels for 0% -> 0%
where the time goes in v1:
time: 1530 us; the launch traced here: 1520 us
  waiting for transfers between devices  639 us (42%)
  matrix products  479 us (31%)
  other arithmetic  180 us (12%)
  local copies, waits for them, and re-layouts  169 us (11%)
  blocking collectives  39 us (3%)
  starting transfers between devices  15.3 us (1%)
    dot_general x18, matrix products, product(): return jnp.einsum(form, left, right, precision=lax.Precision.HIGHEST)  479 us
    all_to_all x1, waiting for transfers between devices, on_device(): lax.all_to_all(sent[0], ('px', 'py'), split_axis=0, concat_axis=1, tiled=...  199 us
    all_to_all x1, waiting for transfers between devices, on_device(): lax.all_to_all(sent[0], ('px', 'py'), split_axis=0, concat_axis=2, tiled=...  179 us
    scatter-add x1, other arithmetic, paint(): return empty.at[cell_rows.reshape(-1)].add(weights.reshape(-1))  174 us
    all_to_all x1, waiting for transfers between devices, on_device(): lax.all_to_all(sent[1], ('px', 'py'), split_axis=0, concat_axis=1, tiled=...  142 us
    all_to_all x1, waiting for transfers between devices, on_device(): lax.all_to_all(jnp.stack(jnp.split(sent[1], lax.axis_size(('px', 'py')),...  119 us
    reshape x2, local copies, waits for them, and re-layouts, on_device(): back_imag.reshape(devices_all, slab_planes, rows_x * rows_y)  33.8 us
    reshape x2, local copies, waits for them, and re-layouts, on_device(): back_real.reshape(devices_all, slab_planes, rows_x * rows_y)  33.8 us
  transfers between devices with their start and end apart: 4, of which 4 were waited for; matrix products, arithmetic and copies ran while one was open for 9% of the time, Pallas kernels for 0%

profile of v1, /device:TPU:0, one launch (start us, length us, event | category | flops | bytes accessed | tf_op | source)
XLA Modules:
  0.0 1523.1 jit_solution(17915809104628593932)
XLA Ops:
  42.8 174.5 %scatter_custom_fusion = f32[1769472]{0:T(1024)} fusion(s32[32768]{0:T(1024)S(1)} %bitcast.318, f32[32768]{0:T(1024)S(1)} %select_bitcast_fusion, f32[]{:T(128)} %constant.19.clone.1), kind=kCustom, calls=%fused_computation.47 | custom fusion | flops 32768 | bytes 7077892 | tf_op jit(solution)/shard_map/scatter-add | solution.py:47
  226.1 25.1 %fusion.29 = f32[384,4608]{1,0:T(8,128)S(1)} fusion(f32[4608,384]{1,0:T(8,128)} %reshape.245, f32[4608,384]{1,0:T(8,128)} %bitcast.315), kind=kOutput, calls=%fused_computation.45 | convolution fusion | flops 8156823552 | bytes 21233664 | tf_op jit(solution)/shard_map/az,zk->ka/dot_general | solution.py:12
  251.1 20.5 %convolution_add_fusion.1 = f32[384,4608]{1,0:T(8,128)S(1)} fusion(f32[384,4608]{1,0:T(8,128)S(1)} %fusion.29, f32[4608,384]{1,0:T(8,128)S(1)} %copy-done.6), kind=kOutput, calls=%fused_computation.11 | convolution fusion | flops 8157118464 | bytes 21233664 | tf_op jit(solution)/shard_map/az,zk->ka/dot_general | solution.py:12
  284.9 29.4 %convolution_subtract_fusion.1 = f32[384,4608]{1,0:T(8,128)} fusion(f32[384,4608]{1,0:T(8,128)} %copy-done.3, f32[4608,384]{1,0:T(8,128)} %bitcast.316), kind=kOutput, calls=%fused_computation.12 | convolution fusion | flops 8157118464 | bytes 21233664 | tf_op jit(solution)/shard_map/az,zk->ka/dot_general | solution.py:12
  322.2 119.3 %all-to-all-done.1 = f32[32,1,12,4608]{3,1,2,0:T(1,128)} async-done(((f32[32,1,12,4608]{3,1,2,0:T(1,128)}), f32[32,1,12,4608]{3,1,2,0:T(1,128)}, u32[]{:S(2)}, u32[]{:S(2)}) %all-to-all-start.1) | async-done | bytes 7077920 | tf_op jit(solution)/shard_map/all_to_all | solution.py:83
  474.0 178.7 %all-to-all-done = f32[32,12,4608]{2,1,0:T(8,128)} async-done(((f32[32,12,4608]{2,1,0:T(8,128)}), f32[32,12,4608]{2,1,0:T(8,128)}, u32[]{:S(2)}, u32[]{:S(2)}) %all-to-all-start) | async-done | bytes 7077920 | tf_op jit(solution)/shard_map/all_to_all | solution.py:81
  678.6 26.6 %fusion.53 = f32[12,4,96,384,1]{3,2,4,1,0:T(8,128)} fusion(f32[12,4,8,96,48]{4,3,2,1,0:T(8,128)} %reshape_reshape.3, s32[8,48]{1,0:T(8,128)S(1)} %multiply_add_fusion), kind=kOutput, calls=%fused_computation.69 | convolution fusion | flops 8155348992 | bytes 14157312 | tf_op jit(solution)/shard_map/kiqxl,qlm->kixm/dot_general | solution.py:12
  705.2 27.8 %fusion = f32[12,4,96,384,1]{3,2,4,1,0:T(8,128)} fusion(f32[12,4,8,96,48]{4,3,2,1,0:T(8,128)S(1)} %copy-done, f32[12,4,8,96,48]{4,3,2,1,0:T(8,128)} %reshape_reshape.3, s32[8,48]{1,0:T(8,128)S(1)} %multiply_add_fusion), kind=kOutput, calls=%fused_computation.1 | convolution fusion | flops 8156823552 | bytes 21235200 | tf_op jit(solution)/shard_map/kiqxl,qlm->kixm/dot_general | solution.py:12
  733.0 22.7 %fusion.51 = f32[12,4,96,384,1]{3,2,4,1,0:T(8,128)} fusion(f32[12,4,8,96,48]{4,3,2,1,0:T(8,128)S(1)} %copy-done, s32[8,48]{1,0:T(8,128)S(1)} %multiply_add_fusion), kind=kOutput, calls=%fused_computation.67 | convolution fusion | flops 8155348992 | bytes 14157312 | tf_op jit(solution)/shard_map/kiqxl,qlm->kixm/dot_general | solution.py:12
  755.7 25.3 %fusion.27 = f32[12,384,384,1]{2,1,3,0:T(8,128)S(1)} fusion(f32[12,4,96,384,1]{3,2,4,1,0:T(8,128)} %fusion.53, f32[12,4,96,384,1]{3,2,4,1,0:T(8,128)} %fusion, f32[12,4,96,384,1]{3,2,4,1,0:T(8,128)} %fusion.51, s32[4,96]{1,0:T(4,128)S(1)} %multiply_add_fusion.1), kind=kOutput, calls=%fused_computation.43 | convolution fusion | flops 8160362496 | bytes 28313088 | tf_op jit(solution)/shard_map/kixm,ixn->kmn/dot_general | solution.py:12
  781.0 50.9 %fusion.21 = f32[12,384,384]{2,1,0:T(8,128)S(1)} fusion(f32[12,384,384,1]{2,1,3,0:T(8,128)S(1)} %fusion.27, f32[384]{0:T(512)S(1)} %fusion.229, f32[12,384]{1,0:T(8,128)S(1)} %broadcast_add_fusion, f32[12,4,96,384,1]{3,2,4,1,0:T(8,128)} %fusion.53, f32[12,4,96,384,1]{3,2,4,1,0:T(8,128)S(1)} %copy-done.7, f32[4,96,384,1]{2,1,0,3:T(8,128)S(1)} %fusion.304), kind=kOutput, calls=%fused_computation.33 | convolution fusion | flops 8178499584 | bytes 28921344 | tf_op jit(solution)/shard_map/kixm,ixn->kmn/dot_general | solution.py:12
  832.0 20.6 %fusion.11 = f32[12,384,4,96]{1,3,2,0:T(8,128)} fusion(f32[12,384,384]{2,1,0:T(8,128)S(1)} %fusion.21, s32[4,96]{1,0:T(4,128)S(1)} %multiply_add_fusion.1), kind=kOutput, calls=%fused_computation.22 | convolution fusion | flops 8155201536 | bytes 14157312 | tf_op jit(solution)/shard_map/kmn,ixn->kmix/dot_general | solution.py:12
  852.5 50.6 %fusion.22 = f32[12,384,384]{2,1,0:T(8,128)S(1)} fusion(f32[12,384,384,1]{2,1,3,0:T(8,128)} %copy-done.9, f32[384]{0:T(512)S(1)} %fusion.229, f32[12,384]{1,0:T(8,128)S(1)} %broadcast_add_fusion, f32[12,4,96,384,1]{3,2,4,1,0:T(8,128)S(1)} %bitcast.312, f32[12,4,96,384,1]{3,2,4,1,0:T(8,128)S(1)} %copy-done.7, f32[4,96,384,1]{2,1,0,3:T(8,128)S(1)} %fusion.306), kind=kOutput, calls=%fused_computation.35 | convolution fusion | flops 8178499584 | bytes 28921344 | tf_op jit(solution)/shard_map/kixm,ixn->kmn/dot_general | solution.py:12
  920.8 19.9 %fusion.9 = f32[12,384,4,96]{1,3,2,0:T(8,128)S(1)} fusion(f32[12,384,384]{2,1,0:T(8,128)} %copy-done.8, s32[4,96]{1,0:T(4,128)S(1)} %multiply_add_fusion.1), kind=kOutput, calls=%fused_computation.20 | convolution fusion | flops 8155201536 | bytes 14157312 | tf_op jit(solution)/shard_map/kmn,ixn->kmix/dot_general | solution.py:12
  940.7 24.2 %fusion.19 = f32[8,48,12,4,96]{4,1,3,2,0:T(8,128)S(1)} fusion(f32[12,384,4,96]{1,3,2,0:T(8,128)S(1)} %fusion.13, f32[12,384,4,96]{1,3,2,0:T(8,128)S(1)} %fusion.9, f32[12,384,4,96]{1,3,2,0:T(8,128)} %fusion.11, s32[8,48]{1,0:T(8,128)S(1)} %multiply_add_fusion), kind=kOutput, calls=%fused_computation.30 | convolution fusion | flops 8160362496 | bytes 28313088 | tf_op jit(solution)/shard_map/kmix,qlm->iqkxl/dot_general | solution.py:12
  968.6 25.1 %add_bitcast_fusion = f32[4,8,12,96,48]{3,4,0,2,1:T(8,128)} fusion(f32[8,48,12,4,96]{4,1,3,2,0:T(8,128)S(1)} %fusion.19, f32[12,384,4,96]{1,3,2,0:T(8,128)S(1)} %fusion.13, f32[12,384,4,96]{1,3,2,0:T(8,128)} %fusion.11, s32[8,48]{1,0:T(8,128)S(1)} %multiply_add_fusion), kind=kOutput, calls=%fused_computation.5 | convolution fusion | flops 8158740480 | bytes 28313088 | tf_op jit(solution)/shard_map/kmix,qlm->iqkxl/dot_general | solution.py:12
  1008.5 19.0 %reshape.299 = f32[32,12,4608]{2,1,0:T(8,128)} reshape(f32[4,8,12,96,48]{4,3,2,1,0:T(8,128)} %copy.46) | data formatting | bytes 14155776 | tf_op jit(solution)/shard_map/reshape | solution.py:106
  1031.4 31.1 %subtract_bitcast_fusion = f32[4,8,12,96,48]{3,4,0,2,1:T(8,128)} fusion(f32[8,48,12,4,96]{4,1,3,2,0:T(8,128)} %copy-done.4, f32[12,384,4,96]{1,3,2,0:T(8,128)} %copy-done.2, f32[12,384,4,96]{1,3,2,0:T(8,128)} %copy-done.5, s32[8,48]{1,0:T(8,128)S(1)} %multiply_add_fusion), kind=kOutput, calls=%fused_computation.6 | convolution fusion | flops 8158740480 | bytes 28313088 | tf_op jit(solution)/shard_map/kmix,qlm->iqkxl/dot_general | solution.py:12
  1077.3 19.0 %reshape.298 = f32[32,12,4608]{2,1,0:T(8,128)} reshape(f32[4,8,12,96,48]{4,3,2,1,0:T(8,128)} %copy.45) | data formatting | bytes 14155776 | tf_op jit(solution)/shard_map/reshape | solution.py:105
  1096.3 142.4 %all-to-all-done.3 = f32[32,12,4608]{2,1,0:T(8,128)} async-done(((f32[32,12,4608]{2,1,0:T(8,128)}), f32[32,12,4608]{2,1,0:T(8,128)}, u32[]{:S(2)}, u32[]{:S(2)}) %all-to-all-start.3) | async-done | bytes 7077920 | tf_op jit(solution)/shard_map/all_to_all | solution.py:110
  1250.6 199.0 %all-to-all-done.2 = f32[32,12,4608]{2,1,0:T(8,128)} async-done(((f32[32,12,4608]{2,1,0:T(8,128)}), f32[32,12,4608]{2,1,0:T(8,128)}, u32[]{:S(2)}, u32[]{:S(2)}) %all-to-all-start.2) | async-done | bytes 7077920 | tf_op jit(solution)/shard_map/all_to_all | solution.py:109
  1457.8 24.1 %fusion.23 = f32[4608,384]{1,0:T(8,128)S(1)} fusion(f32[384,4608]{1,0:T(8,128)} %reshape.251, f32[384,4608]{1,0:T(8,128)} %reshape.253), kind=kOutput, calls=%fused_computation.39 | convolution fusion | flops 8156823552 | bytes 21233664 | tf_op jit(solution)/shard_map/ka,kz->az/dot_general | solution.py:12
  1481.9 18.6 %fusion.4 = f32[4608,384]{1,0:T(8,128)S(1)} fusion(f32[4608,384]{1,0:T(8,128)S(1)} %fusion.23, f32[384,4608]{1,0:T(8,128)S(1)} %copy-done.1), kind=kOutput, calls=%fused_computation.15 | convolution fusion | flops 8160509952 | bytes 21233664 | tf_op jit(solution)/shard_map/ka,kz->az/dot_general | solution.py:12
  1500.6 22.3 %divide_clamp_fusion = f32[4608,384]{1,0:T(8,128)} fusion(f32[4608,384]{1,0:T(8,128)S(1)} %fusion.4, f32[4608,384]{1,0:T(8,128)S(1)} %fusion.23, f32[384,4608]{1,0:T(8,128)S(1)} %bitcast.314), kind=kOutput, calls=%fused_computation.38 | convolution fusion | flops 8162279424 | bytes 28311552 | tf_op jit(solution)/shard_map/ka,kz->az/dot_general | solution.py:12
  (96 shorter events, 204.9 us)
Async XLA Ops:
  226.1 25.1 %copy-start.6 = (f32[4608,384]{1,0:T(8,128)S(1)}, f32[4608,384]{1,0:T(8,128)}, u32[]{:S(2)}) copy-start(f32[4608,384]{1,0:T(8,128)} %reshape.245) | copy-start | bytes 21233668
  251.1 20.5 %copy-start.3 = (f32[384,4608]{1,0:T(8,128)}, f32[384,4608]{1,0:T(8,128)S(1)}, u32[]{:S(2)}) copy-start(f32[384,4608]{1,0:T(8,128)S(1)} %fusion.29) | copy-start | bytes 21233668
  281.1 160.5 %all-to-all-start.1 = ((f32[32,1,12,4608]{3,1,2,0:T(1,128)}), f32[32,1,12,4608]{3,1,2,0:T(1,128)}, u32[]{:S(2)}, u32[]{:S(2)}) async-start(f32[32,1,12,4608]{3,1,2,0:T(1,128)} %copy.18), calls=%async_computation.1 | async-start | bytes 14155776 | tf_op jit(solution)/shard_map/all_to_all | solution.py:83
  441.6 211.2 %all-to-all-start = ((f32[32,12,4608]{2,1,0:T(8,128)}), f32[32,12,4608]{2,1,0:T(8,128)}, u32[]{:S(2)}, u32[]{:S(2)}) async-start(f32[32,12,4608]{2,1,0:T(8,128)} %reshape.247), calls=%async_computation | async-start | bytes 18874368 | tf_op jit(solution)/shard_map/all_to_all | solution.py:81
  678.6 26.6 %copy-start = (f32[12,4,8,96,48]{4,3,2,1,0:T(8,128)S(1)}, f32[12,4,8,96,48]{4,3,2,1,0:T(8,128)}, u32[]{:S(2)}) copy-start(f32[12,4,8,96,48]{4,3,2,1,0:T(8,128)} %reshape.248) | copy-start | bytes 21233668
  755.7 25.3 %copy-start.7 = (f32[12,4,96,384,1]{3,2,4,1,0:T(8,128)S(1)}, f32[12,4,96,384,1]{3,2,4,1,0:T(8,128)}, u32[]{:S(2)}) copy-start(f32[12,4,96,384,1]{3,2,4,1,0:T(8,128)} %fusion) | copy-start | bytes 21233668
  755.7 96.9 %slice-start = ((s8[7077888]{0:T(1024)(128)(4,1)}), s8[4194304]{0:T(1024)(128)(4,1)S(1)}, s32[]{:S(2)}) async-start(s8[7077888]{0:T(1024)(128)(4,1)} %bitcast.311), calls=%async_computation.4 | async-start | bytes 8388608
  781.0 51.0 %copy-start.9 = (f32[12,384,384,1]{2,1,3,0:T(8,128)}, f32[12,384,384,1]{2,1,3,0:T(8,128)S(1)}, u32[]{:S(2)}) copy-start(f32[12,384,384,1]{2,1,3,0:T(8,128)S(1)} %fusion.27) | copy-start | bytes 21233668
  781.0 71.5 %slice-start.1 = ((s8[7077888]{0:T(1024)(128)(4,1)}), s8[2883584]{0:T(1024)(128)(4,1)S(1)}, s32[]{:S(2)}) async-start(s8[7077888]{0:T(1024)(128)(4,1)} %bitcast.311), calls=%async_computation.5 | async-start | bytes 5767168
  903.1 3.0 copy-start.8
  920.8 44.2 %copy-start.2 = (f32[12,384,4,96]{1,3,2,0:T(8,128)}, f32[12,384,4,96]{1,3,2,0:T(8,128)S(1)}, u32[]{:S(2)}) copy-start(f32[12,384,4,96]{1,3,2,0:T(8,128)S(1)} %fusion.13) | copy-start | bytes 21233668
  940.7 24.3 %copy-start.5 = (f32[12,384,4,96]{1,3,2,0:T(8,128)}, f32[12,384,4,96]{1,3,2,0:T(8,128)S(1)}, u32[]{:S(2)}) copy-start(f32[12,384,4,96]{1,3,2,0:T(8,128)S(1)} %fusion.9) | copy-start | bytes 21233668
  965.0 3.7 copy-start.4
  1027.5 211.1 %all-to-all-start.3 = ((f32[32,12,4608]{2,1,0:T(8,128)}), f32[32,12,4608]{2,1,0:T(8,128)}, u32[]{:S(2)}, u32[]{:S(2)}) async-start(f32[32,12,4608]{2,1,0:T(8,128)} %reshape.299), calls=%async_computation.3 | async-start | bytes 18874368 | tf_op jit(solution)/shard_map/all_to_all | solution.py:110
  1238.7 211.0 %all-to-all-start.2 = ((f32[32,12,4608]{2,1,0:T(8,128)}), f32[32,12,4608]{2,1,0:T(8,128)}, u32[]{:S(2)}, u32[]{:S(2)}) async-start(f32[32,12,4608]{2,1,0:T(8,128)} %reshape.298), calls=%async_computation.2 | async-start | bytes 18874368 | tf_op jit(solution)/shard_map/all_to_all | solution.py:109
  1457.8 24.1 %copy-start.1 = (f32[384,4608]{1,0:T(8,128)S(1)}, f32[384,4608]{1,0:T(8,128)}, u32[]{:S(2)}) copy-start(f32[384,4608]{1,0:T(8,128)} %reshape.251) | copy-start | bytes 21233668
  1457.8 42.7 %slice-start.2 = ((s8[7077888]{0:T(1024)(128)(4,1)}), s8[4194304]{0:T(1024)(128)(4,1)S(1)}, s32[]{:S(2)}) async-start(s8[7077888]{0:T(1024)(128)(4,1)} %bitcast.313), calls=%async_computation.6 | async-start | bytes 8388608
  1481.9 18.6 %slice-start.3 = ((s8[7077888]{0:T(1024)(128)(4,1)}), s8[2883584]{0:T(1024)(128)(4,1)S(1)}, s32[]{:S(2)}) async-start(s8[7077888]{0:T(1024)(128)(4,1)} %bitcast.313), calls=%async_computation.7 | async-start | bytes 5767168
